TPU v7x, 32 devices: a whole 2x2x4 slice. The times are simulated.
32 devices in a mesh: dp: 8 (over z, y), tensor: 4 (over x, core).
Axes of the slice: x: 2, y: 2, z: 4, core: 2. Of those that a mesh axis runs over, the one named last changes fastest.
Arguments:
- tokens: bfloat16 [37632, 768], P(('dp', 'tensor')), may hold values from -21 to 21
- res_class: int32 [192], P('dp'), may hold values from 0 to 1
- gain_attn: float32 [768], replicated, may hold values from 0.5 to 1.5
- shift_attn: float32 [768], replicated, may hold values from -1.5 to 1.5
- w_qkv: bfloat16 [768, 3, 768], P(None, None, 'tensor'), may hold values from -0.3125 to 0.3125
- bias_qv: float32 [2, 768], P(None, 'tensor'), may hold values from -1.5 to 1.5
- w_out: bfloat16 [768, 768], P('tensor'), may hold values from -0.625 to 0.625
- bias_out: float32 [768], replicated, may hold values from -1.5 to 1.5
- gain_mlp: float32 [768], replicated, may hold values from 0.5 to 1.5
- shift_mlp: float32 [768], replicated, may hold values from -1.5 to 1.5
- w_up: bfloat16 [768, 3072], P(None, 'tensor'), may hold values from -0.21875 to 0.21875
- bias_up: float32 [3072], P('tensor'), may hold values from -1.5 to 1.5
- w_down: bfloat16 [3072, 768], P('tensor'), may hold values from -0.15625 to 0.15625
- bias_down: float32 [768], replicated, may hold values from -1.5 to 1.5
- cotangent: bfloat16 [37632, 768], P(('dp', 'tensor')), may hold values from -21 to 21
Outputs:
- block_out: bfloat16 [37632, 768], P(('dp', 'tensor'))
- grad_tokens: float32 [37632, 768], P(('dp', 'tensor'))
- grad_gain_attn: float32 [768], replicated
- grad_shift_attn: float32 [768], replicated
- grad_qkv: float32 [768, 3, 768], P(None, None, 'tensor')
- grad_bias_qv: float32 [2, 768], P(None, 'tensor')
- grad_out: float32 [768, 768], P('tensor')
- grad_bias_out: float32 [768], replicated
- grad_gain_mlp: float32 [768], replicated
- grad_shift_mlp: float32 [768], replicated
- grad_up: float32 [768, 3072], P(None, 'tensor')
- grad_bias_up: float32 [3072], P('tensor')
- grad_down: float32 [3072, 768], P('tensor')
- grad_bias_down: float32 [768], replicated
- rms: float32 [3], replicated
All inputs are finite; a program needn't handle non-finite values.
Results may differ from a plain program's by a relative error of at most 0.017.
Values may be sent and summed in bfloat16 or wider, within the bound.
A program may use at most 256 MiB of HBM per device.

v0:
```python
import jax
import jax.numpy as jnp
from jax import lax
from jax.sharding import PartitionSpec as P

HEAD_DIM = 64
PATCHES = 196
PATCHES_LOW = 144
EPS = 1e-06


def normalize(values):
    mean = jnp.mean(values, axis=-1, keepdims=True)
    centred = values - mean
    factor = lax.rsqrt(jnp.mean(centred * centred, axis=-1, keepdims=True) + EPS)
    return (centred * factor, factor)


def norm_back(grad_out, gain, normed, factor):
    scaled = grad_out * gain
    return factor * (
        scaled
        - jnp.mean(scaled, axis=-1, keepdims=True)
        - normed * jnp.mean(scaled * normed, axis=-1, keepdims=True)
    )


def exact_gelu(values):
    return jax.nn.gelu(values, approximate=False)


def on_device(
    tokens,
    res_class,
    gain_attn,
    shift_attn,
    w_qkv,
    bias_qv,
    w_out,
    bias_out,
    gain_mlp,
    shift_mlp,
    w_up,
    bias_up,
    w_down,
    bias_down,
    cotangent,
):
    rows = tokens.shape[0]
    width = tokens.shape[1]
    images = res_class.shape[0]
    local = w_qkv.shape[2]
    heads_here = local // HEAD_DIM
    scale = HEAD_DIM ** (-0.5)
    place = lax.axis_index("tensor")
    counts = jnp.where(res_class == 0, PATCHES, PATCHES_LOW)
    key_valid = jnp.arange(PATCHES)[None, :] < counts[:, None]
    flat_valid = key_valid.reshape(-1).astype(jnp.float32)
    row_valid = lax.dynamic_slice_in_dim(flat_valid, place * rows, rows)[:, None]
    mask = key_valid[:, None, None, :]
    shape = (images, PATCHES, heads_here, HEAD_DIM)
    w_qkv_flat = w_qkv.reshape(width, 3 * local)
    inputs = tokens.astype(jnp.float32)
    normed_a, factor_a = normalize(inputs)
    in_attn = (normed_a * gain_attn + shift_attn).astype(jnp.bfloat16)
    full_attn = lax.all_gather(in_attn, "tensor", axis=0, tiled=True)
    qkv = jnp.dot(full_attn, w_qkv_flat, preferred_element_type=jnp.float32).reshape(-1, 3, local)
    query = (qkv[:, 0] + bias_qv[0]).astype(jnp.bfloat16).reshape(shape)
    keys = qkv[:, 1].astype(jnp.bfloat16).reshape(shape)
    values = (qkv[:, 2] + bias_qv[1]).astype(jnp.bfloat16).reshape(shape)
    scores = jnp.einsum("iqhd,ikhd->ihqk", query, keys, preferred_element_type=jnp.float32) * scale
    scores = jnp.where(mask, scores, -1e30)
    log_total = jax.nn.logsumexp(scores, axis=-1, keepdims=True)
    probs = jnp.exp(scores - log_total).astype(jnp.bfloat16)
    context = (
        jnp.einsum("ihqk,ikhd->iqhd", probs, values, preferred_element_type=jnp.float32)
        .reshape(-1, local)
        .astype(jnp.bfloat16)
    )
    piece = context
    branch = (
        lax.psum_scatter(
            jnp.dot(piece, w_out, preferred_element_type=jnp.float32).astype(jnp.bfloat16),
            "tensor",
            scatter_dimension=0,
            tiled=True,
        ).astype(jnp.float32)
        + bias_out
    )
    hidden = inputs + branch
    normed_m, factor_m = normalize(hidden)
    in_mlp = (normed_m * gain_mlp + shift_mlp).astype(jnp.bfloat16)
    full_mlp = lax.all_gather(in_mlp, "tensor", axis=0, tiled=True)
    pre_act = jnp.dot(full_mlp, w_up, preferred_element_type=jnp.float32) + bias_up
    act = exact_gelu(pre_act).astype(jnp.bfloat16)
    piece = act
    mlp = (
        lax.psum_scatter(
            jnp.dot(piece, w_down, preferred_element_type=jnp.float32).astype(jnp.bfloat16),
            "tensor",
            scatter_dimension=0,
            tiled=True,
        ).astype(jnp.float32)
        + bias_down
    )
    stream = (hidden + mlp) * row_valid
    block_out = stream.astype(jnp.bfloat16)
    grad_stream = cotangent.astype(jnp.float32) * row_valid
    grad_bias_down = jnp.sum(grad_stream, axis=0)
    grad_mlp_full = lax.all_gather(grad_stream.astype(jnp.bfloat16), "tensor", axis=0, tiled=True)
    weight_down = jnp.einsum("tf,td->fd", act, grad_mlp_full, preferred_element_type=jnp.float32)
    grad_act = jnp.einsum("td,fd->tf", grad_mlp_full, w_down, preferred_element_type=jnp.float32)
    gelu_out, gelu_back = jax.vjp(exact_gelu, pre_act)
    grad_pre = gelu_back(grad_act)[0]
    grad_bias_up = jnp.sum(grad_pre, axis=0)
    grad_pre_low = grad_pre.astype(jnp.bfloat16)
    weight_up = jnp.einsum("td,tf->df", full_mlp, grad_pre_low, preferred_element_type=jnp.float32)
    piece = grad_pre_low
    grad_in_mlp = lax.psum_scatter(
        jnp.einsum("tf,df->td", piece, w_up, preferred_element_type=jnp.float32).astype(
            jnp.bfloat16
        ),
        "tensor",
        scatter_dimension=0,
        tiled=True,
    ).astype(jnp.float32)
    grad_gain_mlp = jnp.sum(grad_in_mlp * normed_m, axis=0)
    grad_shift_mlp = jnp.sum(grad_in_mlp, axis=0)
    grad_hidden = grad_stream + norm_back(grad_in_mlp, gain_mlp, normed_m, factor_m)
    grad_bias_out = jnp.sum(grad_hidden, axis=0)
    grad_branch_full = lax.all_gather(
        grad_hidden.astype(jnp.bfloat16), "tensor", axis=0, tiled=True
    )
    weight_out = jnp.einsum(
        "tc,td->cd", context, grad_branch_full, preferred_element_type=jnp.float32
    )
    grad_context = (
        jnp.einsum("td,cd->tc", grad_branch_full, w_out, preferred_element_type=jnp.float32)
        .astype(jnp.bfloat16)
        .reshape(shape)
    )
    again = jnp.einsum("iqhd,ikhd->ihqk", query, keys, preferred_element_type=jnp.float32) * scale
    again = jnp.where(mask, again, -1e30)
    probs_full = jnp.exp(again - log_total)
    probs_low = probs_full.astype(jnp.bfloat16)
    grad_value = jnp.einsum(
        "ihqk,iqhd->ikhd", probs_low, grad_context, preferred_element_type=jnp.float32
    )
    grad_probs = jnp.einsum(
        "iqhd,ikhd->ihqk", grad_context, values, preferred_element_type=jnp.float32
    )
    row_dot = jnp.sum(probs_full * grad_probs, axis=-1, keepdims=True)
    grad_scores = (probs_full * (grad_probs - row_dot)).astype(jnp.bfloat16)
    grad_query = scale * jnp.einsum(
        "ihqk,ikhd->iqhd", grad_scores, keys, preferred_element_type=jnp.float32
    )
    grad_key = scale * jnp.einsum(
        "ihqk,iqhd->ikhd", grad_scores, query, preferred_element_type=jnp.float32
    )
    query_low = grad_query.reshape(-1, local).astype(jnp.bfloat16)
    key_low = grad_key.reshape(-1, local).astype(jnp.bfloat16)
    value_low = grad_value.reshape(-1, local).astype(jnp.bfloat16)
    grad_bias_qv = jnp.stack(
        [
            jnp.sum(query_low.astype(jnp.float32), axis=0),
            jnp.sum(value_low.astype(jnp.float32), axis=0),
        ]
    )
    grad_qkv_low = jnp.stack([query_low, key_low, value_low], axis=1).reshape(-1, 3 * local)
    weight_qkv = jnp.einsum(
        "td,tc->dc", full_attn, grad_qkv_low, preferred_element_type=jnp.float32
    ).reshape(width, 3, local)
    piece = grad_qkv_low
    grad_in_attn = lax.psum_scatter(
        jnp.einsum("tc,dc->td", piece, w_qkv_flat, preferred_element_type=jnp.float32).astype(
            jnp.bfloat16
        ),
        "tensor",
        scatter_dimension=0,
        tiled=True,
    ).astype(jnp.float32)
    grad_gain_attn = jnp.sum(grad_in_attn * normed_a, axis=0)
    grad_shift_attn = jnp.sum(grad_in_attn, axis=0)
    grad_tokens = grad_hidden + norm_back(grad_in_attn, gain_attn, normed_a, factor_a)
    totals = jnp.stack(
        [
            jnp.sum(stream * stream),
            jnp.sum(branch * branch * row_valid),
            jnp.sum(mlp * mlp * row_valid),
            jnp.sum(row_valid),
        ]
    )
    summed = lax.psum(
        (
            grad_gain_attn,
            grad_shift_attn,
            grad_bias_out,
            grad_gain_mlp,
            grad_shift_mlp,
            grad_bias_down,
            totals,
        ),
        ("dp", "tensor"),
    )
    weight_qkv, grad_bias_qv, weight_out, weight_up, grad_bias_up, weight_down = lax.psum(
        (weight_qkv, grad_bias_qv, weight_out, weight_up, grad_bias_up, weight_down), "dp"
    )
    sums = summed[6]
    rms = jnp.sqrt(sums[:3] / (sums[3] * width))
    return (
        block_out,
        grad_tokens,
        summed[0],
        summed[1],
        weight_qkv,
        grad_bias_qv,
        weight_out,
        summed[2],
        summed[3],
        summed[4],
        weight_up,
        grad_bias_up,
        weight_down,
        summed[5],
        rms,
    )


def solution(mesh):
    in_specs = (
        P(("dp", "tensor"), None),
        P("dp"),
        P(),
        P(),
        P(None, None, "tensor"),
        P(None, "tensor"),
        P("tensor", None),
        P(),
        P(),
        P(),
        P(None, "tensor"),
        P("tensor"),
        P("tensor", None),
        P(),
        P(("dp", "tensor"), None),
    )
    out_specs = (
        P(("dp", "tensor"), None),
        P(("dp", "tensor"), None),
        P(),
        P(),
        P(None, None, "tensor"),
        P(None, "tensor"),
        P("tensor", None),
        P(),
        P(),
        P(),
        P(None, "tensor"),
        P("tensor"),
        P("tensor", None),
        P(),
        P(),
    )
    return jax.shard_map(
        on_device, mesh=mesh, in_specs=in_specs, out_specs=out_specs, check_vma=False
    )
```

profile of v0, /device:TPU:0, one launch (start us, length us, event | category | flops | bytes accessed | tf_op | source)
XLA Modules:
  0.0 985.3 jit_solution(16900257428672392909)
XLA Ops:
  7.3 2.0 convert_reduce_fusion.2
  9.2 2.1 fusion.30
  12.0 2.6 fusion.26
  16.8 52.4 %all-gather.5.cloned.1.call-done = bf16[4704,768]{1,0:T(8,128)(2,1)} async-done(((bf16[1176,768]{1,0:T(8,128)(2,1)}), bf16[4704,768]{1,0:T(8,128)(2,1)}) %all-gather.5.cloned.1.call-update) | async-done | bytes 7225360 | tf_op jit(solution)/shard_map/all_gather | solution.py:66
  69.2 7.3 fusion.10
  76.5 1.4 slice.36
  77.9 3.4 fusion.73
  81.4 6.0 convert_element_type.155
  87.4 6.4 squeeze.9
  93.9 6.4 squeeze.8
  100.3 7.4 fusion.6
  108.3 4.7 exponential_reduce_fusion
  114.0 11.1 %convert_bitcast_fusion = bf16[24,196,3,64]{1,3,2,0:T(8,128)(2,1)S(1)} fusion(f32[24,196,3,64]{1,0,3,2:T(8,128)} %squeeze.8, f32[3,64]{1,0:T(4,128)} %add.138, f32[24,3,196,196]{2,3,1,0:T(8,128)} %copy-done.2, f32[24,3,196]{2,1,0:T(4,128)S(1)} %log_add_fusion, pred[24,196]{1,0:T(8,128)(4,1)S(1)} %get-tuple-element.54), kind=kOutput, calls=%fused_computation.91 | convolution fusion | flops 367815168 | bytes 16544736 | tf_op jit(solution)/shard_map/ihqk,ikhd->iqhd/dot_general | solution.py:76
  125.1 2.7 copy.44
  127.9 4.7 convert_element_type.159
  132.6 6.5 convolution_convert_fusion.2
  140.7 63.8 %reduce-scatter.5.cloned.1.call-done = bf16[1176,768]{1,0:T(8,128)(2,1)} async-done(((bf16[4704,768]{1,0:T(8,128)(2,1)}), bf16[1176,768]{1,0:T(8,128)(2,1)}) %reduce-scatter.5.cloned.1.call-update) | async-done | bytes 1806352 | tf_op jit(solution)/shard_map/reduce_scatter | solution.py:82
  204.5 2.3 fusion.60
  207.1 4.9 multiply_reduce_fusion.2
  212.5 2.2 add_convert_fusion
  215.4 51.2 %all-gather.7.cloned.1.call-done = bf16[4704,768]{1,0:T(8,128)(2,1)} async-done(((bf16[1176,768]{1,0:T(8,128)(2,1)}), bf16[4704,768]{1,0:T(8,128)(2,1)}) %all-gather.7.cloned.1.call-update) | async-done | bytes 7225360 | tf_op jit(solution)/shard_map/all_gather | solution.py:93
  266.6 11.9 %fusion.74 = f32[4704,768]{1,0:T(8,128)} fusion(bf16[4704,768]{1,0:T(8,128)(2,1)} %all-gather.7.cloned.1.call-done, bf16[768,768]{1,0:T(8,128)(2,1)} %param.25), kind=kOutput, calls=%fused_computation.132 | convolution fusion | flops 5549064192 | bytes 22855680 | tf_op jit(solution)/shard_map/dot_general | solution.py:94
  278.5 41.8 %all-gather.9.cloned.1.call-done = bf16[4704,768]{1,0:T(8,128)(2,1)} async-done(((bf16[1176,768]{1,0:T(8,128)(2,1)}), bf16[4704,768]{1,0:T(8,128)(2,1)}) %all-gather.9.cloned.1.call-update) | async-done | bytes 7225360 | tf_op jit(solution)/shard_map/all_gather | solution.py:110
  320.3 41.0 %fusion.68 = (f32[768]{0:T(1024)S(1)}, bf16[4704,768]{1,0:T(8,128)(2,1)}, f32[4704,768]{1,0:T(8,128)S(1)}) fusion(f32[4704,768]{1,0:T(8,128)} %fusion.74, f32[768]{0:T(1024)S(1)} %copy-done.50, bf16[4704,768]{1,0:T(8,128)(2,1)} %all-gather.9.cloned.1.call-done, bf16[768,768]{1,0:T(8,128)(2,1)S(1)} %copy-done), kind=kOutput, calls=%fused_computation.128 | convolution fusion | flops 5816400896 | bytes 44537856 | tf_op jit(solution)/shard_map/td,fd->tf/dot_general | solution.py:112
  361.3 4.3 multiply_convert_fusion.1
  365.6 10.8 %convolution_convert_fusion.1 = bf16[4704,768]{1,0:T(8,128)(2,1)} fusion(bf16[4704,768]{1,0:T(8,128)(2,1)} %multiply_convert_fusion.1, bf16[768,768]{1,0:T(8,128)(2,1)S(1)} %copy-done), kind=kOutput, calls=%fused_computation.25 | convolution fusion | flops 5552676864 | bytes 15630336 | tf_op jit(solution)/shard_map/dot_general | solution.py:99
  377.7 11.2 %convolution_convert_fusion = bf16[4704,768]{1,0:T(8,128)(2,1)} fusion(bf16[768,768]{1,0:T(8,128)(2,1)S(1)} %copy-done.54, bf16[4704,768]{1,0:T(8,128)(2,1)} %get-tuple-element.43), kind=kOutput, calls=%fused_computation.24 | convolution fusion | flops 5552676864 | bytes 15630336 | tf_op jit(solution)/shard_map/tf,df->td/dot_general | solution.py:120
  389.1 52.8 %reduce-scatter.7.cloned.1.call-done = bf16[1176,768]{1,0:T(8,128)(2,1)} async-done(((bf16[4704,768]{1,0:T(8,128)(2,1)}), bf16[1176,768]{1,0:T(8,128)(2,1)}) %reduce-scatter.7.cloned.1.call-update) | async-done | bytes 1806352 | tf_op jit(solution)/shard_map/reduce_scatter | solution.py:98
  441.8 67.6 %reduce-scatter.9.cloned.1.call-done = bf16[1176,768]{1,0:T(8,128)(2,1)} async-done(((bf16[4704,768]{1,0:T(8,128)(2,1)}), bf16[1176,768]{1,0:T(8,128)(2,1)}) %reduce-scatter.9.cloned.1.call-update) | async-done | bytes 1806352 | tf_op jit(solution)/shard_map/reduce_scatter | solution.py:119
  509.5 8.3 fusion.36
  517.9 2.3 fusion.71
  520.2 1.8 copy-done.10
  523.5 51.8 %all-gather.11.cloned.1.call-done = bf16[4704,768]{1,0:T(8,128)(2,1)} async-done(((bf16[1176,768]{1,0:T(8,128)(2,1)}), bf16[4704,768]{1,0:T(8,128)(2,1)}) %all-gather.11.cloned.1.call-update) | async-done | bytes 7225360 | tf_op jit(solution)/shard_map/all_gather | solution.py:131
  575.3 6.8 convolution_convert_fusion.3
  582.1 6.2 reshape.193
  588.3 9.9 %convert_reduce_fusion.3 = (f32[3,64]{1,0:T(4,128)S(1)}, bf16[24,3,64,196]{3,2,1,0:T(8,128)(2,1)}) fusion(f32[24,3,196,196]{2,3,1,0:T(8,128)} %copy-done.2, f32[24,3,196]{2,1,0:T(4,128)S(1)} %copy-done.24, pred[24,196]{1,0:T(8,128)(4,1)S(1)} %copy-done.30, bf16[24,196,3,64]{1,0,3,2:T(8,128)(2,1)} %reshape.193), kind=kOutput, calls=%fused_computation.53 | convolution fusion | flops 367814976 | bytes 14738400 | tf_op jit(solution)/shard_map/ihqk,iqhd->ikhd/dot_general | solution.py:146
  599.8 11.2 %multiply_reduce_fusion = (f32[24,3,196]{2,1,0:T(4,128)S(1)}, f32[24,3,196,196]{2,3,1,0:T(8,128)}) fusion(f32[24,3,196,196]{2,3,1,0:T(8,128)S(1)} %bitcast.79, f32[24,3,196]{2,1,0:T(4,128)S(1)} %copy-done.24, pred[24,196]{1,0:T(8,128)(4,1)S(1)} %copy-done.30, f32[24,196,3,64]{1,0,3,2:T(8,128)} %squeeze.8, f32[3,64]{1,0:T(4,128)S(1)} %copy-done.47, ...), kind=kOutput, calls=%fused_computation.2 | convolution fusion | flops 369663840 | bytes 27664992 | tf_op jit(solution)/shard_map/iqhd,ikhd->ihqk/dot_general | solution.py:149
  611.0 10.2 %multiply_convert_fusion = bf16[24,3,196,196]{2,3,1,0:T(8,128)(2,1)} fusion(f32[24,3,196,196]{2,3,1,0:T(8,128)} %get-tuple-element.59, f32[24,3,196,196]{2,3,1,0:T(8,128)S(1)} %bitcast.79, f32[24,3,196]{2,1,0:T(4,128)S(1)} %get-tuple-element.58, f32[24,3,196]{2,1,0:T(4,128)S(1)} %copy-done.24, pred[24,196]{1,0:T(8,128)(4,1)S(1)} %copy-done.30), kind=kLoop, calls=%fused_computation.1 | loop fusion | flops 16595712 | bytes 27777120 | tf_op jit(solution)/shard_map/convert_element_type | solution.py:153
  621.2 8.7 fusion.43
  630.0 2.9 convert_reduce_fusion.4
  632.9 2.8 copy.53
  635.7 4.7 convert_element_type.185
  640.5 2.7 copy.48
  643.2 4.7 convert_element_type.179
  647.9 3.0 copy.50
  650.9 3.0 convert_element_type.182
  654.0 1.8 constant_dynamic-update-slice_fusion.2
  656.8 2.3 copy-done.26
  659.1 7.9 bitcast_convert_fusion
  667.1 11.8 %fusion.38 = f32[768,768]{1,0:T(8,128)} fusion(bf16[4704,768]{1,0:T(8,128)(2,1)} %all-gather.7.cloned.1.call-done, bf16[4704,768]{1,0:T(8,128)(2,1)} %get-tuple-element.43), kind=kOutput, calls=%fused_computation.78 | convolution fusion | flops 5549064192 | bytes 16809984 | tf_op jit(solution)/shard_map/td,tf->df/dot_general | solution.py:117
  678.9 12.2 %fusion.76 = f32[768,768]{1,0:T(8,128)} fusion(bf16[4704,768]{1,0:T(8,128)(2,1)} %multiply_convert_fusion.1, bf16[4704,768]{1,0:T(8,128)(2,1)} %all-gather.9.cloned.1.call-done), kind=kOutput, calls=%fused_computation.134 | convolution fusion | flops 5549064192 | bytes 16809984 | tf_op jit(solution)/shard_map/tf,td->fd/dot_general | solution.py:111
  691.1 2.5 fusion.75
  693.6 5.9 fusion.8
  699.6 2.8 pad_maximum_fusion.1
  702.6 22.3 %all-reduce.1 = (f32[2,192]{1,0:T(2,128)}, f32[768]{0:T(1024)}) all-reduce(f32[2,192]{1,0:T(2,128)S(1)} %pad_maximum_fusion, f32[768]{0:T(1024)S(1)} %get-tuple-element.42), channel_id=1, replica_groups=mesh['dp'=8,'tensor'=4] {'dp'}, use_global_device_ids=true, to_apply=%region_22.23 | all-reduce | flops 1152 | bytes 9216 | tf_op jit(solution)/shard_map/psum | solution.py:205
  724.8 7.6 reduce-scatter.11.cloned.1.call-done
  732.4 3.4 fusion.37
  735.8 44.5 %all-reduce = (f32[768]{0:T(1024)}, f32[768]{0:T(1024)}, f32[768]{0:T(1024)}, f32[768]{0:T(1024)}, f32[768]{0:T(1024)}, /*index=5*/f32[768]{0:T(1024)}, f32[4]{0:T(128)S(1)}) all-reduce(f32[768]{0:T(1024)S(1)} %get-tuple-element.17, f32[768]{0:T(1024)S(1)} %get-tuple-element.25, ...), channel_id=1, replica_groups=mesh['dp'=8,'tensor'=4] {'dp','tensor'}, use_global_device_ids=true, to_apply=%region_16.17 | all-reduce | flops 4612 | bytes 36896 | tf_op jit(solution)/shard_map/psum | solution.py:193
  782.1 4.6 fusion.29
  786.7 183.9 %all-reduce.5.cloned.1.call-done = (f32[768,3,192]{0,2,1:T(8,128)}, f32[192,768]{1,0:T(8,128)}, f32[768,768]{1,0:T(8,128)}, f32[768,768]{1,0:T(8,128)}) async-done(((f32[768,3,192]{0,2,1:T(8,128)}, f32[192,768]{1,0:T(8,128)}, f32[768,768]{1,0:T(8,128)}, f32[768,768]{1,0:T(8,128)}), (f32[768,3,192]{0,2,1:T(8,128)}, f32[192,768]{1,0:T(8,128)}, f32[768,768]{1,0:T(8,128)}, ...) | async-done | bytes 7077904 | tf_op jit(solution)/shard_map/psum | solution.py:205
  970.6 2.9 copy.96
  973.6 2.0 copy.97
  975.6 1.4 copy.98
  977.0 1.4 copy.99
  (178 shorter events, 14.3 us)
Async XLA Ops:
  7.2 313.1 %copy-start = (bf16[768,768]{1,0:T(8,128)(2,1)S(1)}, bf16[768,768]{1,0:T(8,128)(2,1)}, u32[]{:S(2)}) copy-start(bf16[768,768]{1,0:T(8,128)(2,1)} %param.27) | copy-start | bytes 3538948
  7.2 4.8 copy-start.3
  7.2 7.5 copy-start.53
  7.2 8.9 copy-start.56
  7.2 62.0 %all-gather.5.cloned.1.call-start = ((), (), s32[]{:S(2)}) async-start(), calls=%async_computation.4 | async-start | bytes 9031680 | tf_op jit(solution)/shard_map/all_gather | solution.py:66
  14.7 189.8 %reduce-scatter.5.cloned.1.call-start = ((), (), s32[]{:S(2)}) async-start(), calls=%async_computation.5 | async-start | bytes 9031680 | tf_op jit(solution)/shard_map/reduce_scatter | solution.py:82
  16.8 97.2 %copy-start.29 = (pred[24,196]{1,0:T(8,128)(4,1)}, pred[24,196]{1,0:T(8,128)(4,1)S(1)}, u32[]{:S(2)}) copy-start(pred[24,196]{1,0:T(8,128)(4,1)S(1)} %get-tuple-element.54) | copy-start | bytes 14116
  107.7 5.3 copy-start.2
  114.0 11.1 %copy-start.23 = (f32[24,3,196]{2,1,0:T(4,128)}, f32[24,3,196]{2,1,0:T(4,128)S(1)}, u32[]{:S(2)}) copy-start(f32[24,3,196]{2,1,0:T(4,128)S(1)} %log_add_fusion) | copy-start | bytes 169348
  125.1 7.5 copy-start.27
  139.1 65.4 %copy-start.41 = (f32[768]{0:T(1024)S(1)}, f32[768]{0:T(1024)}, u32[]{:S(2)}) copy-start(f32[768]{0:T(1024)} %param.22) | copy-start | bytes 9220
  139.1 127.5 %all-gather.7.cloned.1.call-start = ((), (), s32[]{:S(2)}) async-start(), calls=%async_computation.6 | async-start | bytes 9031680 | tf_op jit(solution)/shard_map/all_gather | solution.py:93
  140.7 71.3 %copy-start.37 = (f32[1176]{0:T(1024)}, f32[1176]{0:T(1024)S(1)}, u32[]{:S(2)}) copy-start(f32[1176]{0:T(1024)S(1)} %get-tuple-element.46) | copy-start | bytes 14116
  140.7 71.9 %copy-start.44 = (f32[768]{0:T(1024)S(1)}, f32[768]{0:T(1024)}, u32[]{:S(2)}) copy-start(f32[768]{0:T(1024)} %param.23) | copy-start | bytes 9220
  140.7 71.9 %copy-start.52 = (f32[768]{0:T(1024)S(1)}, f32[768]{0:T(1024)}, u32[]{:S(2)}) copy-start(f32[768]{0:T(1024)} %param.24) | copy-start | bytes 9220
  206.8 5.1 copy-start.33
  214.8 105.5 %all-gather.9.cloned.1.call-start = ((), (), s32[]{:S(2)}) async-start(), calls=%async_computation.8 | async-start | bytes 9031680 | tf_op jit(solution)/shard_map/all_gather | solution.py:110
  215.4 104.9 %copy-start.50 = (f32[768]{0:T(1024)S(1)}, f32[768]{0:T(1024)}, u32[]{:S(2)}) copy-start(f32[768]{0:T(1024)} %param.26) | copy-start | bytes 9220
  215.4 226.5 %reduce-scatter.7.cloned.1.call-start = ((), (), s32[]{:S(2)}) async-start(), calls=%async_computation.7 | async-start | bytes 9031680 | tf_op jit(solution)/shard_map/reduce_scatter | solution.py:98
  320.3 41.1 %copy-start.13 = (f32[4704,768]{1,0:T(8,128)S(1)}, f32[4704,768]{1,0:T(8,128)}, u32[]{:S(2)}) copy-start(f32[4704,768]{1,0:T(8,128)} %fusion.74) | copy-start | bytes 43352068
  376.5 133.0 %reduce-scatter.9.cloned.1.call-start = ((), (), s32[]{:S(2)}) async-start(), calls=%async_computation.9 | async-start | bytes 9031680 | tf_op jit(solution)/shard_map/reduce_scatter | solution.py:119
  389.0 120.5 %copy-start.4 = (bf16[1176,768]{1,0:T(8,128)(2,1)S(1)}, bf16[1176,768]{1,0:T(8,128)(2,1)}, u32[]{:S(2)}) copy-start(bf16[1176,768]{1,0:T(8,128)(2,1)} %param.15) | copy-start | bytes 5419012
  389.0 120.5 %copy-start.34 = (f32[1176]{0:T(1024)S(1)}, f32[1176]{0:T(1024)}, u32[]{:S(2)}) copy-start(f32[1176]{0:T(1024)} %copy-done.33) | copy-start | bytes 14116
  389.0 120.5 %copy-start.38 = (f32[1176]{0:T(1024)S(1)}, f32[1176]{0:T(1024)}, u32[]{:S(2)}) copy-start(f32[1176]{0:T(1024)} %copy-done.37) | copy-start | bytes 14116
  389.0 120.5 %copy-start.40 = (f32[1176]{0:T(1024)S(1)}, f32[1176]{0:T(1024)}, u32[]{:S(2)}) copy-start(f32[1176]{0:T(1024)} %copy-done.39) | copy-start | bytes 14116
  389.0 120.5 %copy-start.42 = (f32[768]{0:T(1024)S(1)}, f32[768]{0:T(1024)}, u32[]{:S(2)}) copy-start(f32[768]{0:T(1024)} %param.22) | copy-start | bytes 9220
  389.0 120.5 %copy-start.45 = (f32[768]{0:T(1024)S(1)}, f32[768]{0:T(1024)}, u32[]{:S(2)}) copy-start(f32[768]{0:T(1024)} %param.23) | copy-start | bytes 9220
  389.0 120.5 %copy-start.51 = (f32[768]{0:T(1024)S(1)}, f32[768]{0:T(1024)}, u32[]{:S(2)}) copy-start(f32[768]{0:T(1024)} %param.28) | copy-start | bytes 9220
  389.0 186.2 %all-gather.11.cloned.1.call-start = ((), (), s32[]{:S(2)}) async-start(), calls=%async_computation.10 | async-start | bytes 9031680 | tf_op jit(solution)/shard_map/all_gather | solution.py:131
  509.5 8.3 copy-start.8
  509.5 8.3 copy-start.18
  509.5 8.3 copy-start.19
  520.2 55.1 %copy-start.28 = (bf16[192,768]{1,0:T(8,128)(2,1)S(1)}, bf16[192,768]{1,0:T(8,128)(2,1)}, u32[]{:S(2)}) copy-start(bf16[192,768]{1,0:T(8,128)(2,1)} %param.21) | copy-start | bytes 884740
  523.4 64.8 %copy-start.24 = (f32[24,3,196]{2,1,0:T(4,128)S(1)}, f32[24,3,196]{2,1,0:T(4,128)}, u32[]{:S(2)}) copy-start(f32[24,3,196]{2,1,0:T(4,128)} %copy-done.23) | copy-start | bytes 169348
  523.5 64.8 %copy-start.30 = (pred[24,196]{1,0:T(8,128)(4,1)S(1)}, pred[24,196]{1,0:T(8,128)(4,1)}, u32[]{:S(2)}) copy-start(pred[24,196]{1,0:T(8,128)(4,1)} %copy-done.29) | copy-start | bytes 14116
  523.5 208.9 %reduce-scatter.11.cloned.1.call-start = ((), (), s32[]{:S(2)}) async-start(), calls=%async_computation.11 | async-start | bytes 9031680 | tf_op jit(solution)/shard_map/reduce_scatter | solution.py:174
  582.1 16.2 %slice-start = ((s8[14745600]{0:T(1024)(128)(4,1)}), s8[2162688]{0:T(1024)(128)(4,1)S(1)}, s32[]{:S(2)}) async-start(s8[14745600]{0:T(1024)(128)(4,1)} %bitcast.78), calls=%async_computation.13 | async-start | bytes 4325376
  588.3 10.0 %slice-start.1 = ((s8[14745600]{0:T(1024)(128)(4,1)}), s8[4194304]{0:T(1024)(128)(4,1)S(1)}, s32[]{:S(2)}) async-start(s8[14745600]{0:T(1024)(128)(4,1)} %bitcast.78), calls=%async_computation.14 | async-start | bytes 8388608
  588.3 10.0 %slice-start.2 = ((s8[14745600]{0:T(1024)(128)(4,1)}), s8[4194304]{0:T(1024)(128)(4,1)S(1)}, s32[]{:S(2)}) async-start(s8[14745600]{0:T(1024)(128)(4,1)} %bitcast.78), calls=%async_computation.15 | async-start | bytes 8388608
  588.3 10.9 %slice-start.3 = ((s8[14745600]{0:T(1024)(128)(4,1)}), s8[4194304]{0:T(1024)(128)(4,1)S(1)}, s32[]{:S(2)}) async-start(s8[14745600]{0:T(1024)(128)(4,1)} %bitcast.78), calls=%async_computation.16 | async-start | bytes 8388608
  588.3 11.5 %copy-start.11 = (bf16[24,196,3,64]{1,0,3,2:T(8,128)(2,1)S(1)}, bf16[24,196,3,64]{1,0,3,2:T(8,128)(2,1)}, u32[]{:S(2)}) copy-start(bf16[24,196,3,64]{1,0,3,2:T(8,128)(2,1)} %reshape.193) | copy-start | bytes 5419012
  588.3 11.5 %copy-start.47 = (f32[3,64]{1,0:T(4,128)S(1)}, f32[3,64]{1,0:T(4,128)}, u32[]{:S(2)}) copy-start(f32[3,64]{1,0:T(4,128)} %add.138) | copy-start | bytes 2308
  611.0 10.2 %copy-start.48 = (f32[3,64]{1,0:T(4,128)S(1)}, f32[3,64]{1,0:T(4,128)}, u32[]{:S(2)}) copy-start(f32[3,64]{1,0:T(4,128)} %add.141) | copy-start | bytes 2308
  621.2 8.8 copy-start.6
  621.2 8.8 copy-start.9
  630.0 2.9 copy-start.22
  632.9 7.6 copy-start.12
  654.0 5.1 copy-start.55
  667.1 303.6 %all-reduce.5.cloned.1.call-start = ((), (), s32[]{:S(2)}) async-start(), calls=%async_computation.12 | async-start | bytes 14155776 | tf_op jit(solution)/shard_map/psum | solution.py:205
  667.1 24.0 %slice-start.8 = ((s8[7225344]{0:T(1024)(128)(4,1)}), s8[4194304]{0:T(1024)(128)(4,1)S(1)}, s32[]{:S(2)}) async-start(s8[7225344]{0:T(1024)(128)(4,1)} %bitcast.86), calls=%async_computation.21 | async-start | bytes 8388608
  667.1 26.5 %slice-start.4 = ((s8[5455872]{0:T(1024)(128)(4,1)}), s8[4194304]{0:T(1024)(128)(4,1)S(1)}, s32[]{:S(2)}) async-start(s8[5455872]{0:T(1024)(128)(4,1)} %bitcast.82), calls=%async_computation.17 | async-start | bytes 8388608
  667.1 26.5 %slice-start.6 = ((s8[7225344]{0:T(1024)(128)(4,1)}), s8[4194304]{0:T(1024)(128)(4,1)S(1)}, s32[]{:S(2)}) async-start(s8[7225344]{0:T(1024)(128)(4,1)} %bitcast.84), calls=%async_computation.19 | async-start | bytes 8388608
  678.9 12.2 %copy-start.14 = (bf16[4704,192]{0,1:T(8,128)(2,1)S(1)}, bf16[4704,192]{0,1:T(8,128)(2,1)}, u32[]{:S(2)}) copy-start(bf16[4704,192]{0,1:T(8,128)(2,1)} %convert_element_type.159) | copy-start | bytes 5419012
  678.9 12.2 %slice-start.9 = ((s8[7225344]{0:T(1024)(128)(4,1)}), s8[3031040]{0:T(1024)(128)(4,1)S(1)}, s32[]{:S(2)}) async-start(s8[7225344]{0:T(1024)(128)(4,1)} %bitcast.86), calls=%async_computation.22 | async-start | bytes 6062080
  678.9 14.7 %slice-start.5 = ((s8[5455872]{0:T(1024)(128)(4,1)}), s8[1261568]{0:T(1024)(128)(4,1)S(1)}, s32[]{:S(2)}) async-start(s8[5455872]{0:T(1024)(128)(4,1)} %bitcast.82), calls=%async_computation.18 | async-start | bytes 2523136
  678.9 14.7 %slice-start.7 = ((s8[7225344]{0:T(1024)(128)(4,1)}), s8[3031040]{0:T(1024)(128)(4,1)S(1)}, s32[]{:S(2)}) async-start(s8[7225344]{0:T(1024)(128)(4,1)} %bitcast.84), calls=%async_computation.20 | async-start | bytes 6062080
  699.5 32.8 %copy-start.5 = (bf16[1176,768]{1,0:T(8,128)(2,1)S(1)}, bf16[1176,768]{1,0:T(8,128)(2,1)}, u32[]{:S(2)}) copy-start(bf16[1176,768]{1,0:T(8,128)(2,1)} %param.15) | copy-start | bytes 5419012
  699.5 32.8 %copy-start.32 = (f32[1176]{0:T(1024)S(1)}, f32[1176]{0:T(1024)}, u32[]{:S(2)}) copy-start(f32[1176]{0:T(1024)} %copy-done.31) | copy-start | bytes 14116
  699.5 32.8 %copy-start.36 = (f32[1176]{0:T(1024)S(1)}, f32[1176]{0:T(1024)}, u32[]{:S(2)}) copy-start(f32[1176]{0:T(1024)} %copy-done.35) | copy-start | bytes 14116
  699.6 32.8 %copy-start.46 = (f32[768]{0:T(1024)S(1)}, f32[768]{0:T(1024)}, u32[]{:S(2)}) copy-start(f32[768]{0:T(1024)} %param.17) | copy-start | bytes 9220
  699.6 36.3 %copy-start.49 = (f32[768]{0:T(1024)S(1)}, f32[768]{0:T(1024)}, u32[]{:S(2)}) copy-start(f32[768]{0:T(1024)} %get-tuple-element.26) | copy-start | bytes 9220
  970.6 5.0 copy-start.21
  970.6 6.4 copy-start.20
  973.6 4.8 copy-start.1
  (12 other events, 19.7 us)
Sparse Core Ops, SparseCore 0:
  14.8 54.3 all-gather.4
  139.3 65.1 reduce-scatter.4
  214.9 51.6 all-gather.6
  268.6 51.6 all-gather.8
  376.6 65.1 reduce-scatter.6
  444.3 65.1 reduce-scatter.8
  523.6 51.6 all-gather.10
  667.2 65.1 reduce-scatter.10
  738.0 232.6 all-reduce.4
where the time goes:
time: 995 us; the launch traced here: 985 us
  waiting for transfers between devices  574 us (58%)
  matrix products  187 us (19%)
  local copies, waits for them, and re-layouts  81.1 us (8%)
  blocking collectives  66.7 us (7%)
  other arithmetic  61.1 us (6%)
  between operations  15.5 us (2%)
    psum x1, waiting for transfers between devices, on_device(): lax.psum((weight_qkv, grad_bias_qv, weight_out, weight_up, grad_bias_up,...  184 us
    reduce_scatter x1, waiting for transfers between devices, on_device(): lax.psum_scatter(jnp.einsum('tf,df->td', piece, w_up, preferred_element_t...  67.6 us
    reduce_scatter x1, waiting for transfers between devices, on_device(): lax.psum_scatter(jnp.dot(piece, w_out, preferred_element_type=jnp.float32...  63.8 us
    reduce_scatter x1, waiting for transfers between devices, on_device(): lax.psum_scatter(jnp.dot(piece, w_down, preferred_element_type=jnp.float3...  52.8 us
    all_gather x1, waiting for transfers between devices, on_device(): full_attn = lax.all_gather(in_attn, 'tensor', axis=0, tiled=True)  52.4 us
    all_gather x1, waiting for transfers between devices, on_device(): lax.all_gather(grad_hidden.astype(jnp.bfloat16), 'tensor', axis=0, tiled=...  51.8 us
    all_gather x1, waiting for transfers between devices, on_device(): full_mlp = lax.all_gather(in_mlp, 'tensor', axis=0, tiled=True)  51.2 us
    psum x1, blocking collectives, on_device(): lax.psum((grad_gain_attn, grad_shift_attn, grad_bias_out, grad_gain_mlp,...  44.5 us
  transfers between devices with their start and end apart: 9, of which 9 were waited for; matrix products, arithmetic and copies ran while one was open for 7% of the time, Pallas kernels for 0%

commit v1 on v0

--- a/solution.py
+++ b/solution.py
@@ -7,6 +7,24 @@
 PATCHES = 196
 PATCHES_LOW = 144
 EPS = 1e-06
+
+
+def in_order(pieces, dim):
+    pieces = jnp.moveaxis(pieces, 0, dim)
+    shape = pieces.shape
+    return pieces.reshape(*shape[:dim], shape[dim] * shape[dim + 1], *shape[dim + 2 :])
+
+
+def grow_blocks(value, axis):
+    count = lax.axis_size(axis)
+    pieces = value[None]
+    for level in range(count.bit_length() - 1):
+        bit = 1 << level
+        partner_block = lax.ppermute(pieces, axis, [(i, i ^ bit) for i in range(count)])
+        both = jnp.stack([pieces, partner_block])
+        upper = lax.axis_index(axis) >> level & 1
+        pieces = jnp.where(upper == 0, both, both[::-1]).reshape(-1, *value.shape)
+    return pieces
 
 
 def normalize(values):
@@ -63,7 +81,7 @@
     inputs = tokens.astype(jnp.float32)
     normed_a, factor_a = normalize(inputs)
     in_attn = (normed_a * gain_attn + shift_attn).astype(jnp.bfloat16)
-    full_attn = lax.all_gather(in_attn, "tensor", axis=0, tiled=True)
+    full_attn = in_order(grow_blocks(in_attn, "tensor"), 0)
     qkv = jnp.dot(full_attn, w_qkv_flat, preferred_element_type=jnp.float32).reshape(-1, 3, local)
     query = (qkv[:, 0] + bias_qv[0]).astype(jnp.bfloat16).reshape(shape)
     keys = qkv[:, 1].astype(jnp.bfloat16).reshape(shape)

time: 995 us -> 1040 us (1.045)
  waiting for transfers between devices: 574 us -> 603 us
  other arithmetic: 61.1 us -> 76.2 us
    ppermute x0 -> x2, waiting for transfers between devices: none -> 80.4 us  [grow_blocks(): lax.ppermute(pieces, axis, [(i, i ^ bit) for i in range(count)])]
    all_gather x1 -> x0, waiting for transfers between devices: 52.4 us -> none  [on_device(): full_attn = lax.all_gather(in_attn, 'tensor', axis=0, tiled=True)]
    another operation x0 -> x4, other arithmetic: none -> 13.1 us  [grow_blocks(): both = jnp.stack([pieces, partner_block])]
  transfers between devices with their start and end apart: 9 -> 10, of which waited for: 9 -> 10; matrix products, arithmetic and copies ran while one was open for 7% -> 7% of each run, Pallas kernels for 0% -> 0%
where the time goes in v1:
time: 1040 us; the launch traced here: 1030 us
  waiting for transfers between devices  603 us (58%)
  matrix products  187 us (18%)
  local copies, waits for them, and re-layouts  80.6 us (8%)
  other arithmetic  76.2 us (7%)
  blocking collectives  66.7 us (6%)
  between operations  15.6 us (2%)
    psum x1, waiting for transfers between devices, on_device(): lax.psum((weight_qkv, grad_bias_qv, weight_out, weight_up, grad_bias_up,...  184 us
    ppermute x2, waiting for transfers between devices, grow_blocks(): lax.ppermute(pieces, axis, [(i, i ^ bit) for i in range(count)])  80.4 us
    reduce_scatter x1, waiting for transfers between devices, on_device(): lax.psum_scatter(jnp.einsum('tf,df->td', piece, w_up, preferred_element_t...  67.6 us
    reduce_scatter x1, waiting for transfers between devices, on_device(): lax.psum_scatter(jnp.dot(piece, w_out, preferred_element_type=jnp.float32...  65.3 us
    reduce_scatter x1, waiting for transfers between devices, on_device(): lax.psum_scatter(jnp.dot(piece, w_down, preferred_element_type=jnp.float3...  52.9 us
    all_gather x1, waiting for transfers between devices, on_device(): lax.all_gather(grad_hidden.astype(jnp.bfloat16), 'tensor', axis=0, tiled=...  51.8 us
    all_gather x1, waiting for transfers between devices, on_device(): full_mlp = lax.all_gather(in_mlp, 'tensor', axis=0, tiled=True)  51 us
    psum x1, blocking collectives, on_device(): lax.psum((grad_gain_attn, grad_shift_attn, grad_bias_out, grad_gain_mlp,...  44.5 us
  transfers between devices with their start and end apart: 10, of which 10 were waited for; matrix products, arithmetic and copies ran while one was open for 7% of the time, Pallas kernels for 0%

profile of v1, /device:TPU:0, one launch (start us, length us, event | category | flops | bytes accessed | tf_op | source)
XLA Modules:
  0.0 1032.9 jit_solution(17438708368219831603)
XLA Ops:
  9.2 2.2 fusion.27
  11.4 3.2 fusion.69
  15.2 3.7 collective-permute-done
  18.9 2.4 pad_maximum_fusion.1
  21.3 3.7 fusion.41
  25.0 2.8 collective-permute-start.1
  29.8 76.7 %collective-permute-done.1 = bf16[2,1176,768]{2,1,0:T(8,128)(2,1)} collective-permute-done((bf16[2,1176,768]{2,1,0:T(8,128)(2,1)}, bf16[2,1176,768]{2,1,0:T(8,128)(2,1)}, u32[]{:S(2)}, u32[]{:S(2)}) %collective-permute-start.1) | collective-permute-done | bytes 3612704 | tf_op jit(solution)/shard_map/ppermute | solution.py:23
  106.5 3.8 pad_maximum_fusion
  110.3 4.2 reverse_select_fusion
  114.5 7.2 fusion.54
  123.2 3.5 fusion.75
  126.6 6.0 convert_element_type.155
  132.7 6.4 squeeze.9
  139.1 6.5 squeeze.8
  145.6 7.4 fusion.6
  153.6 4.4 exponential_reduce_fusion
  159.1 11.1 %convert_bitcast_fusion = bf16[24,196,3,64]{1,3,2,0:T(8,128)(2,1)S(1)} fusion(f32[24,196,3,64]{1,0,3,2:T(8,128)} %squeeze.8, f32[3,64]{1,0:T(4,128)} %add.138, f32[24,3,196,196]{2,3,1,0:T(8,128)} %copy-done.2, f32[24,3,196]{2,1,0:T(4,128)S(1)} %log_add_fusion, pred[24,196]{1,0:T(8,128)(4,1)S(1)} %get-tuple-element.58), kind=kOutput, calls=%fused_computation.94 | convolution fusion | flops 367815168 | bytes 16544736 | tf_op jit(solution)/shard_map/ihqk,ikhd->iqhd/dot_general | solution.py:94
  170.2 2.7 copy.44
  172.9 4.8 convert_element_type.159
  177.7 6.5 convolution_convert_fusion.2
  185.7 65.3 %reduce-scatter.5.cloned.1.call-done = bf16[1176,768]{1,0:T(8,128)(2,1)} async-done(((bf16[4704,768]{1,0:T(8,128)(2,1)}), bf16[1176,768]{1,0:T(8,128)(2,1)}) %reduce-scatter.5.cloned.1.call-update) | async-done | bytes 1806352 | tf_op jit(solution)/shard_map/reduce_scatter | solution.py:100
  251.0 2.3 fusion.60
  253.6 5.1 multiply_reduce_fusion.2
  259.4 2.2 add_convert_fusion
  262.4 51.0 %all-gather.4.cloned.1.call-done = bf16[4704,768]{1,0:T(8,128)(2,1)} async-done(((bf16[1176,768]{1,0:T(8,128)(2,1)}), bf16[4704,768]{1,0:T(8,128)(2,1)}) %all-gather.4.cloned.1.call-update) | async-done | bytes 7225360 | tf_op jit(solution)/shard_map/all_gather | solution.py:111
  313.4 11.8 %fusion.76 = f32[4704,768]{1,0:T(8,128)} fusion(bf16[4704,768]{1,0:T(8,128)(2,1)} %all-gather.4.cloned.1.call-done, bf16[768,768]{1,0:T(8,128)(2,1)} %param.25), kind=kOutput, calls=%fused_computation.138 | convolution fusion | flops 5549064192 | bytes 22855680 | tf_op jit(solution)/shard_map/dot_general | solution.py:112
  325.2 42.0 %all-gather.6.cloned.1.call-done = bf16[4704,768]{1,0:T(8,128)(2,1)} async-done(((bf16[1176,768]{1,0:T(8,128)(2,1)}), bf16[4704,768]{1,0:T(8,128)(2,1)}) %all-gather.6.cloned.1.call-update) | async-done | bytes 7225360 | tf_op jit(solution)/shard_map/all_gather | solution.py:128
  367.3 41.1 %fusion.70 = (f32[768]{0:T(1024)S(1)}, bf16[4704,768]{1,0:T(8,128)(2,1)}, f32[4704,768]{1,0:T(8,128)S(1)}) fusion(f32[4704,768]{1,0:T(8,128)} %fusion.76, f32[768]{0:T(1024)S(1)} %copy-done.50, bf16[4704,768]{1,0:T(8,128)(2,1)} %all-gather.6.cloned.1.call-done, bf16[768,768]{1,0:T(8,128)(2,1)S(1)} %copy-done), kind=kOutput, calls=%fused_computation.134 | convolution fusion | flops 5816400896 | bytes 44537856 | tf_op jit(solution)/shard_map/td,fd->tf/dot_general | solution.py:130
  408.4 4.5 multiply_convert_fusion.1
  412.8 10.8 %convolution_convert_fusion.1 = bf16[4704,768]{1,0:T(8,128)(2,1)} fusion(bf16[4704,768]{1,0:T(8,128)(2,1)} %multiply_convert_fusion.1, bf16[768,768]{1,0:T(8,128)(2,1)S(1)} %copy-done), kind=kOutput, calls=%fused_computation.26 | convolution fusion | flops 5552676864 | bytes 15630336 | tf_op jit(solution)/shard_map/dot_general | solution.py:117
  424.9 11.1 %convolution_convert_fusion = bf16[4704,768]{1,0:T(8,128)(2,1)} fusion(bf16[768,768]{1,0:T(8,128)(2,1)S(1)} %copy-done.54, bf16[4704,768]{1,0:T(8,128)(2,1)} %get-tuple-element.43), kind=kOutput, calls=%fused_computation.25 | convolution fusion | flops 5552676864 | bytes 15630336 | tf_op jit(solution)/shard_map/tf,df->td/dot_general | solution.py:138
  436.1 52.9 %reduce-scatter.7.cloned.1.call-done = bf16[1176,768]{1,0:T(8,128)(2,1)} async-done(((bf16[4704,768]{1,0:T(8,128)(2,1)}), bf16[1176,768]{1,0:T(8,128)(2,1)}) %reduce-scatter.7.cloned.1.call-update) | async-done | bytes 1806352 | tf_op jit(solution)/shard_map/reduce_scatter | solution.py:116
  489.0 67.6 %reduce-scatter.9.cloned.1.call-done = bf16[1176,768]{1,0:T(8,128)(2,1)} async-done(((bf16[4704,768]{1,0:T(8,128)(2,1)}), bf16[1176,768]{1,0:T(8,128)(2,1)}) %reduce-scatter.9.cloned.1.call-update) | async-done | bytes 1806352 | tf_op jit(solution)/shard_map/reduce_scatter | solution.py:137
  556.7 8.3 fusion.33
  565.0 2.3 fusion.73
  570.6 51.8 %all-gather.8.cloned.1.call-done = bf16[4704,768]{1,0:T(8,128)(2,1)} async-done(((bf16[1176,768]{1,0:T(8,128)(2,1)}), bf16[4704,768]{1,0:T(8,128)(2,1)}) %all-gather.8.cloned.1.call-update) | async-done | bytes 7225360 | tf_op jit(solution)/shard_map/all_gather | solution.py:149
  622.4 6.8 convolution_convert_fusion.3
  629.2 6.2 reshape.197
  635.5 9.9 convert_reduce_fusion.3
  647.0 11.2 %multiply_reduce_fusion = (f32[24,3,196]{2,1,0:T(4,128)S(1)}, f32[24,3,196,196]{2,3,1,0:T(8,128)}) fusion(f32[24,3,196,196]{2,3,1,0:T(8,128)S(1)} %bitcast.89, f32[24,3,196]{2,1,0:T(4,128)S(1)} %copy-done.24, pred[24,196]{1,0:T(8,128)(4,1)S(1)} %copy-done.30, f32[24,196,3,64]{1,0,3,2:T(8,128)} %squeeze.8, f32[3,64]{1,0:T(4,128)S(1)} %copy-done.47, ...), kind=kOutput, calls=%fused_computation.2 | convolution fusion | flops 369663840 | bytes 27664992 | tf_op jit(solution)/shard_map/iqhd,ikhd->ihqk/dot_general | solution.py:167
  658.1 10.4 %multiply_convert_fusion = bf16[24,3,196,196]{2,3,1,0:T(8,128)(2,1)} fusion(f32[24,3,196,196]{2,3,1,0:T(8,128)} %get-tuple-element.63, f32[24,3,196,196]{2,3,1,0:T(8,128)S(1)} %bitcast.89, f32[24,3,196]{2,1,0:T(4,128)S(1)} %get-tuple-element.62, f32[24,3,196]{2,1,0:T(4,128)S(1)} %copy-done.24, pred[24,196]{1,0:T(8,128)(4,1)S(1)} %copy-done.30), kind=kLoop, calls=%fused_computation.1 | loop fusion | flops 16595712 | bytes 27777120 | tf_op jit(solution)/shard_map/convert_element_type | solution.py:171
  668.6 8.7 fusion.42
  677.3 2.9 convert_reduce_fusion.4
  680.3 2.8 copy.53
  683.1 4.7 convert_element_type.185
  687.8 2.7 copy.48
  690.6 4.7 convert_element_type.179
  695.3 3.0 copy.50
  698.3 3.0 convert_element_type.182
  704.2 2.3 copy-done.26
  706.5 8.0 bitcast_convert_fusion
  714.5 11.7 %fusion.35 = f32[768,768]{1,0:T(8,128)} fusion(bf16[4704,768]{1,0:T(8,128)(2,1)} %all-gather.4.cloned.1.call-done, bf16[4704,768]{1,0:T(8,128)(2,1)} %get-tuple-element.43), kind=kOutput, calls=%fused_computation.79 | convolution fusion | flops 5549064192 | bytes 16809984 | tf_op jit(solution)/shard_map/td,tf->df/dot_general | solution.py:135
  726.3 12.2 %fusion.78 = f32[768,768]{1,0:T(8,128)} fusion(bf16[4704,768]{1,0:T(8,128)(2,1)} %multiply_convert_fusion.1, bf16[4704,768]{1,0:T(8,128)(2,1)} %all-gather.6.cloned.1.call-done), kind=kOutput, calls=%fused_computation.140 | convolution fusion | flops 5549064192 | bytes 16809984 | tf_op jit(solution)/shard_map/tf,td->fd/dot_general | solution.py:129
  738.5 2.5 fusion.77
  741.0 5.9 fusion.8
  747.0 2.8 pad_maximum_fusion.3
  749.9 22.2 %all-reduce.1 = (f32[2,192]{1,0:T(2,128)}, f32[768]{0:T(1024)}) all-reduce(f32[2,192]{1,0:T(2,128)S(1)} %pad_maximum_fusion.2, f32[768]{0:T(1024)S(1)} %get-tuple-element.42), channel_id=1, replica_groups=mesh['dp'=8,'tensor'=4] {'dp'}, use_global_device_ids=true, to_apply=%region_22.23 | all-reduce | flops 1152 | bytes 9216 | tf_op jit(solution)/shard_map/psum | solution.py:223
  772.2 7.6 reduce-scatter.11.cloned.1.call-done
  779.8 3.4 fusion.34
  783.2 44.5 %all-reduce = (f32[768]{0:T(1024)}, f32[768]{0:T(1024)}, f32[768]{0:T(1024)}, f32[768]{0:T(1024)}, f32[768]{0:T(1024)}, /*index=5*/f32[768]{0:T(1024)}, f32[4]{0:T(128)S(1)}) all-reduce(f32[768]{0:T(1024)S(1)} %get-tuple-element.17, f32[768]{0:T(1024)S(1)} %get-tuple-element.25, ...), channel_id=1, replica_groups=mesh['dp'=8,'tensor'=4] {'dp','tensor'}, use_global_device_ids=true, to_apply=%region_16.17 | all-reduce | flops 4612 | bytes 36896 | tf_op jit(solution)/shard_map/psum | solution.py:211
  829.5 4.6 fusion.26
  834.1 183.9 %all-reduce.5.cloned.1.call-done = (f32[768,3,192]{0,2,1:T(8,128)}, f32[192,768]{1,0:T(8,128)}, f32[768,768]{1,0:T(8,128)}, f32[768,768]{1,0:T(8,128)}) async-done(((f32[768,3,192]{0,2,1:T(8,128)}, f32[192,768]{1,0:T(8,128)}, f32[768,768]{1,0:T(8,128)}, f32[768,768]{1,0:T(8,128)}), (f32[768,3,192]{0,2,1:T(8,128)}, f32[192,768]{1,0:T(8,128)}, f32[768,768]{1,0:T(8,128)}, ...) | async-done | bytes 7077904 | tf_op jit(solution)/shard_map/psum | solution.py:223
  1018.0 2.9 copy.96
  1021.0 2.0 copy.97
  (185 shorter events, 24.1 us)
Async XLA Ops:
  7.2 360.1 %copy-start = (bf16[768,768]{1,0:T(8,128)(2,1)S(1)}, bf16[768,768]{1,0:T(8,128)(2,1)}, u32[]{:S(2)}) copy-start(bf16[768,768]{1,0:T(8,128)(2,1)} %param.27) | copy-start | bytes 3538948
  7.2 4.2 copy-start.3
  7.2 243.8 %reduce-scatter.5.cloned.1.call-start = ((), (), s32[]{:S(2)}) async-start(), calls=%async_computation.4 | async-start | bytes 9031680 | tf_op jit(solution)/shard_map/reduce_scatter | solution.py:100
  14.7 4.2 collective-permute-start
  21.2 6.6 copy-start.53
  21.3 7.9 copy-start.57
  25.0 81.6 %collective-permute-start.1 = (bf16[2,1176,768]{2,1,0:T(8,128)(2,1)}, bf16[2,1176,768]{2,1,0:T(8,128)(2,1)}, u32[]{:S(2)}, u32[]{:S(2)}) collective-permute-start(bf16[2,1176,768]{2,1,0:T(8,128)(2,1)} %get-tuple-element.53), channel_id=1, source_target_pairs={{0,2},{1,3},{2,0},{3,1},{4,6},{5,7},{6,4},{7,5},{8,10},{9,11},{10,... | collective-permute-start | bytes 10838024 | tf_op jit(solution)/shard_map/ppermute | solution.py:23
  29.8 129.2 %copy-start.29 = (pred[24,196]{1,0:T(8,128)(4,1)}, pred[24,196]{1,0:T(8,128)(4,1)S(1)}, u32[]{:S(2)}) copy-start(pred[24,196]{1,0:T(8,128)(4,1)S(1)} %get-tuple-element.58) | copy-start | bytes 14116
  152.9 5.2 copy-start.2
  159.0 11.1 %copy-start.23 = (f32[24,3,196]{2,1,0:T(4,128)}, f32[24,3,196]{2,1,0:T(4,128)S(1)}, u32[]{:S(2)}) copy-start(f32[24,3,196]{2,1,0:T(4,128)S(1)} %log_add_fusion) | copy-start | bytes 169348
  170.2 7.5 copy-start.27
  184.2 66.8 %copy-start.41 = (f32[768]{0:T(1024)S(1)}, f32[768]{0:T(1024)}, u32[]{:S(2)}) copy-start(f32[768]{0:T(1024)} %param.22) | copy-start | bytes 9220
  184.2 129.2 %all-gather.4.cloned.1.call-start = ((), (), s32[]{:S(2)}) async-start(), calls=%async_computation.5 | async-start | bytes 9031680 | tf_op jit(solution)/shard_map/all_gather | solution.py:111
  185.7 73.0 %copy-start.37 = (f32[1176]{0:T(1024)}, f32[1176]{0:T(1024)S(1)}, u32[]{:S(2)}) copy-start(f32[1176]{0:T(1024)S(1)} %get-tuple-element.46) | copy-start | bytes 14116
  185.7 73.6 %copy-start.44 = (f32[768]{0:T(1024)S(1)}, f32[768]{0:T(1024)}, u32[]{:S(2)}) copy-start(f32[768]{0:T(1024)} %param.23) | copy-start | bytes 9220
  185.7 73.6 %copy-start.52 = (f32[768]{0:T(1024)S(1)}, f32[768]{0:T(1024)}, u32[]{:S(2)}) copy-start(f32[768]{0:T(1024)} %param.24) | copy-start | bytes 9220
  253.4 5.4 copy-start.33
  261.6 105.6 %all-gather.6.cloned.1.call-start = ((), (), s32[]{:S(2)}) async-start(), calls=%async_computation.7 | async-start | bytes 9031680 | tf_op jit(solution)/shard_map/all_gather | solution.py:128
  262.4 104.9 %copy-start.50 = (f32[768]{0:T(1024)S(1)}, f32[768]{0:T(1024)}, u32[]{:S(2)}) copy-start(f32[768]{0:T(1024)} %param.26) | copy-start | bytes 9220
  262.4 226.6 %reduce-scatter.7.cloned.1.call-start = ((), (), s32[]{:S(2)}) async-start(), calls=%async_computation.6 | async-start | bytes 9031680 | tf_op jit(solution)/shard_map/reduce_scatter | solution.py:116
  367.3 41.1 %copy-start.13 = (f32[4704,768]{1,0:T(8,128)S(1)}, f32[4704,768]{1,0:T(8,128)}, u32[]{:S(2)}) copy-start(f32[4704,768]{1,0:T(8,128)} %fusion.76) | copy-start | bytes 43352068
  423.7 132.9 %reduce-scatter.9.cloned.1.call-start = ((), (), s32[]{:S(2)}) async-start(), calls=%async_computation.8 | async-start | bytes 9031680 | tf_op jit(solution)/shard_map/reduce_scatter | solution.py:137
  436.0 120.6 %copy-start.4 = (bf16[1176,768]{1,0:T(8,128)(2,1)S(1)}, bf16[1176,768]{1,0:T(8,128)(2,1)}, u32[]{:S(2)}) copy-start(bf16[1176,768]{1,0:T(8,128)(2,1)} %param.15) | copy-start | bytes 5419012
  436.0 120.6 %copy-start.34 = (f32[1176]{0:T(1024)S(1)}, f32[1176]{0:T(1024)}, u32[]{:S(2)}) copy-start(f32[1176]{0:T(1024)} %copy-done.33) | copy-start | bytes 14116
  436.0 120.6 %copy-start.38 = (f32[1176]{0:T(1024)S(1)}, f32[1176]{0:T(1024)}, u32[]{:S(2)}) copy-start(f32[1176]{0:T(1024)} %copy-done.37) | copy-start | bytes 14116
  436.0 120.6 %copy-start.40 = (f32[1176]{0:T(1024)S(1)}, f32[1176]{0:T(1024)}, u32[]{:S(2)}) copy-start(f32[1176]{0:T(1024)} %copy-done.39) | copy-start | bytes 14116
  436.0 120.6 %copy-start.42 = (f32[768]{0:T(1024)S(1)}, f32[768]{0:T(1024)}, u32[]{:S(2)}) copy-start(f32[768]{0:T(1024)} %param.22) | copy-start | bytes 9220
  436.0 120.6 %copy-start.45 = (f32[768]{0:T(1024)S(1)}, f32[768]{0:T(1024)}, u32[]{:S(2)}) copy-start(f32[768]{0:T(1024)} %param.23) | copy-start | bytes 9220
  436.0 120.6 %copy-start.51 = (f32[768]{0:T(1024)S(1)}, f32[768]{0:T(1024)}, u32[]{:S(2)}) copy-start(f32[768]{0:T(1024)} %param.28) | copy-start | bytes 9220
  436.0 186.3 %all-gather.8.cloned.1.call-start = ((), (), s32[]{:S(2)}) async-start(), calls=%async_computation.9 | async-start | bytes 9031680 | tf_op jit(solution)/shard_map/all_gather | solution.py:149
  556.6 8.3 copy-start.8
  556.6 8.3 copy-start.18
  556.7 8.3 copy-start.19
  567.3 55.1 %copy-start.28 = (bf16[192,768]{1,0:T(8,128)(2,1)S(1)}, bf16[192,768]{1,0:T(8,128)(2,1)}, u32[]{:S(2)}) copy-start(bf16[192,768]{1,0:T(8,128)(2,1)} %param.21) | copy-start | bytes 884740
  570.6 64.8 %copy-start.24 = (f32[24,3,196]{2,1,0:T(4,128)S(1)}, f32[24,3,196]{2,1,0:T(4,128)}, u32[]{:S(2)}) copy-start(f32[24,3,196]{2,1,0:T(4,128)} %copy-done.23) | copy-start | bytes 169348
  570.6 64.8 %copy-start.30 = (pred[24,196]{1,0:T(8,128)(4,1)S(1)}, pred[24,196]{1,0:T(8,128)(4,1)}, u32[]{:S(2)}) copy-start(pred[24,196]{1,0:T(8,128)(4,1)} %copy-done.29) | copy-start | bytes 14116
  570.6 209.2 %reduce-scatter.11.cloned.1.call-start = ((), (), s32[]{:S(2)}) async-start(), calls=%async_computation.10 | async-start | bytes 9031680 | tf_op jit(solution)/shard_map/reduce_scatter | solution.py:192
  629.2 16.2 %slice-start = ((s8[14745600]{0:T(1024)(128)(4,1)}), s8[2162688]{0:T(1024)(128)(4,1)S(1)}, s32[]{:S(2)}) async-start(s8[14745600]{0:T(1024)(128)(4,1)} %bitcast.88), calls=%async_computation.12 | async-start | bytes 4325376
  635.4 10.0 slice-start.1
  635.4 10.0 slice-start.2
  635.4 10.9 %slice-start.3 = ((s8[14745600]{0:T(1024)(128)(4,1)}), s8[4194304]{0:T(1024)(128)(4,1)S(1)}, s32[]{:S(2)}) async-start(s8[14745600]{0:T(1024)(128)(4,1)} %bitcast.88), calls=%async_computation.15 | async-start | bytes 8388608
  635.4 11.5 %copy-start.11 = (bf16[24,196,3,64]{1,0,3,2:T(8,128)(2,1)S(1)}, bf16[24,196,3,64]{1,0,3,2:T(8,128)(2,1)}, u32[]{:S(2)}) copy-start(bf16[24,196,3,64]{1,0,3,2:T(8,128)(2,1)} %reshape.197) | copy-start | bytes 5419012
  635.4 11.5 %copy-start.47 = (f32[3,64]{1,0:T(4,128)S(1)}, f32[3,64]{1,0:T(4,128)}, u32[]{:S(2)}) copy-start(f32[3,64]{1,0:T(4,128)} %add.138) | copy-start | bytes 2308
  658.1 10.4 %copy-start.48 = (f32[3,64]{1,0:T(4,128)S(1)}, f32[3,64]{1,0:T(4,128)}, u32[]{:S(2)}) copy-start(f32[3,64]{1,0:T(4,128)} %add.141) | copy-start | bytes 2308
  668.6 8.8 copy-start.6
  668.6 8.8 copy-start.9
  680.3 7.6 copy-start.12
  701.3 5.1 copy-start.56
  714.5 303.6 %all-reduce.5.cloned.1.call-start = ((), (), s32[]{:S(2)}) async-start(), calls=%async_computation.11 | async-start | bytes 14155776 | tf_op jit(solution)/shard_map/psum | solution.py:223
  714.5 23.9 %slice-start.8 = ((s8[7225344]{0:T(1024)(128)(4,1)}), s8[4194304]{0:T(1024)(128)(4,1)S(1)}, s32[]{:S(2)}) async-start(s8[7225344]{0:T(1024)(128)(4,1)} %bitcast.98), calls=%async_computation.20 | async-start | bytes 8388608
  714.5 26.5 %slice-start.4 = ((s8[7225344]{0:T(1024)(128)(4,1)}), s8[4194304]{0:T(1024)(128)(4,1)S(1)}, s32[]{:S(2)}) async-start(s8[7225344]{0:T(1024)(128)(4,1)} %bitcast.92), calls=%async_computation.16 | async-start | bytes 8388608
  714.5 26.5 %slice-start.6 = ((s8[5455872]{0:T(1024)(128)(4,1)}), s8[4194304]{0:T(1024)(128)(4,1)S(1)}, s32[]{:S(2)}) async-start(s8[5455872]{0:T(1024)(128)(4,1)} %bitcast.96), calls=%async_computation.18 | async-start | bytes 8388608
  726.3 12.2 %copy-start.14 = (bf16[4704,192]{0,1:T(8,128)(2,1)S(1)}, bf16[4704,192]{0,1:T(8,128)(2,1)}, u32[]{:S(2)}) copy-start(bf16[4704,192]{0,1:T(8,128)(2,1)} %convert_element_type.159) | copy-start | bytes 5419012
  726.3 12.2 %slice-start.9 = ((s8[7225344]{0:T(1024)(128)(4,1)}), s8[3031040]{0:T(1024)(128)(4,1)S(1)}, s32[]{:S(2)}) async-start(s8[7225344]{0:T(1024)(128)(4,1)} %bitcast.98), calls=%async_computation.21 | async-start | bytes 6062080
  726.3 14.7 %slice-start.5 = ((s8[7225344]{0:T(1024)(128)(4,1)}), s8[3031040]{0:T(1024)(128)(4,1)S(1)}, s32[]{:S(2)}) async-start(s8[7225344]{0:T(1024)(128)(4,1)} %bitcast.92), calls=%async_computation.17 | async-start | bytes 6062080
  726.3 14.7 %slice-start.7 = ((s8[5455872]{0:T(1024)(128)(4,1)}), s8[1261568]{0:T(1024)(128)(4,1)S(1)}, s32[]{:S(2)}) async-start(s8[5455872]{0:T(1024)(128)(4,1)} %bitcast.96), calls=%async_computation.19 | async-start | bytes 2523136
  746.9 32.9 %copy-start.5 = (bf16[1176,768]{1,0:T(8,128)(2,1)S(1)}, bf16[1176,768]{1,0:T(8,128)(2,1)}, u32[]{:S(2)}) copy-start(bf16[1176,768]{1,0:T(8,128)(2,1)} %param.15) | copy-start | bytes 5419012
  746.9 32.9 %copy-start.32 = (f32[1176]{0:T(1024)S(1)}, f32[1176]{0:T(1024)}, u32[]{:S(2)}) copy-start(f32[1176]{0:T(1024)} %copy-done.31) | copy-start | bytes 14116
  746.9 32.9 %copy-start.36 = (f32[1176]{0:T(1024)S(1)}, f32[1176]{0:T(1024)}, u32[]{:S(2)}) copy-start(f32[1176]{0:T(1024)} %copy-done.35) | copy-start | bytes 14116
  746.9 32.9 %copy-start.46 = (f32[768]{0:T(1024)S(1)}, f32[768]{0:T(1024)}, u32[]{:S(2)}) copy-start(f32[768]{0:T(1024)} %param.17) | copy-start | bytes 9220
  746.9 36.3 %copy-start.49 = (f32[768]{0:T(1024)S(1)}, f32[768]{0:T(1024)}, u32[]{:S(2)}) copy-start(f32[768]{0:T(1024)} %get-tuple-element.26) | copy-start | bytes 9220
  1018.0 5.0 copy-start.21
  1018.0 6.4 copy-start.20
  1021.0 4.8 copy-start.1
  (14 other events, 29.5 us)
Sparse Core Ops, SparseCore 0:
  184.4 66.6 reduce-scatter.4
  261.8 51.6 all-gather.3
  315.6 51.6 all-gather.5
  423.8 65.1 reduce-scatter.6
  491.4 65.1 reduce-scatter.8
  570.7 51.6 all-gather.7
  714.6 65.1 reduce-scatter.10
  785.4 232.6 all-reduce.4
